TPU v7x, 32 devices: a whole 2x2x4 slice. The times are simulated.
32 devices in a mesh: shard: 4 (over z), ctx: 4 (over y, x), tp: 2 (over core).
Axes of the slice: x: 2, y: 2, z: 4, core: 2. Of those that a mesh axis runs over, the one named last changes fastest.
Arguments:
- hidden_in: bfloat16 [4, 512, 1536], P('shard', 'ctx'), may hold values from -6 to 6
- seg_start: int32 [4, 512], P('shard', 'ctx'), may hold values from 0 to 511, as said below
- norm1_gain: bfloat16 [1536], P('shard'), may hold values from 0.5 to 1.5
- w_qkv: bfloat16 [1536, 2, 8, 128], P('shard', 'tp'), may hold values from -0.15625 to 0.15625
- b_qkv: bfloat16 [128, 2, 8], P('shard', 'tp'), may hold values from -2 to 2
- w_attn_out: bfloat16 [1536, 1536], P('shard', 'tp'), may hold values from -0.875 to 0.875
- norm2_gain: bfloat16 [1536], P('shard'), may hold values from 0.5 to 1.5
- w_gate_up: bfloat16 [1536, 2, 8960], P('shard', None, 'tp'), may hold values from -0.15625 to 0.15625
- w_down: bfloat16 [1536, 8960], P('shard', 'tp'), may hold values from -0.0625 to 0.0625
- out_grad: bfloat16 [4, 512, 1536], P('shard', 'ctx'), may hold values from -6 to 6
Outputs:
- layer_out: float32 [4, 512, 1536], P('shard', 'ctx')
- in_grad: float32 [4, 512, 1536], P('shard', 'ctx')
- grad_norm1: float32 [1536], P('shard')
- grad_qkv: float32 [1536, 2, 8, 128], P('shard', 'tp')
- grad_bias: float32 [128, 2, 8], P('shard', 'tp')
- grad_attn_out: float32 [1536, 1536], P('shard', 'tp')
- grad_norm2: float32 [1536], P('shard')
- grad_gate_up: float32 [1536, 2, 8960], P('shard', None, 'tp')
- grad_down: float32 [1536, 8960], P('shard', 'tp')
Inputs may be any that keep to these rules, and one draw needn't show every extreme that they name: seg_start never falls along a row and equals its own position at a segment's first token; every segment holds 1 to 256 tokens, and every row has a segment of exactly 256 tokens.
All inputs are finite; a program needn't handle non-finite values.
Results may differ from a plain program's by a relative error of at most 0.02.
Values may be sent and summed in bfloat16 or wider, within the bound.
A program may use at most 320 MiB of HBM per device.

v0:
```python
import jax
import jax.numpy as jnp
from jax import lax
from jax.sharding import PartitionSpec as P

EPSILON = 1e-06
ROPE_BASE = 1000000.0
NEGATIVE = -1e30


def rope_tables(positions, head_dim):
    half_dim = head_dim // 2
    frequency = ROPE_BASE ** (-(jnp.arange(half_dim, dtype=jnp.float32) * 2.0) / head_dim)
    angles = positions[:, None] * frequency[None, :]
    cosine = jnp.cos(angles)
    sine_vals = jnp.sin(angles)
    return (jnp.concatenate([cosine, cosine], -1), jnp.concatenate([sine_vals, sine_vals], -1))


def rotate_half(values):
    half_dim = values.shape[-1] // 2
    return jnp.concatenate([-values[..., half_dim:], values[..., :half_dim]], -1)


def rotate_back(values):
    half_dim = values.shape[-1] // 2
    return jnp.concatenate([values[..., half_dim:], -values[..., :half_dim]], -1)


def apply_rope(values, cosine, sine_vals):
    return values * cosine + rotate_half(values) * sine_vals


def rope_grad(grads, cosine, sine_vals):
    return grads * cosine + rotate_back(grads * sine_vals)


def rms_back(grad_norm, inputs, inv_rms, gain_vals):
    scaled = gain_vals * grad_norm
    return inv_rms * scaled - inputs * (inv_rms * inv_rms * inv_rms) * jnp.mean(
        scaled * inputs, -1, keepdims=True
    )


def tensor_sum(partial_sum):
    return lax.psum(partial_sum, "tp")


def contract_rows(left, right):
    return lax.dot_general(
        left, right, (((0,), (0,)), ((), ())), preferred_element_type=jnp.float32
    )


def contract_cols(left, right):
    return lax.dot_general(
        left, right, (((1,), (1,)), ((), ())), preferred_element_type=jnp.float32
    )


def body(
    hidden_in,
    seg_start,
    norm1_gain,
    w_qkv,
    b_qkv,
    w_attn_out,
    norm2_gain,
    w_gate_up,
    w_down,
    out_grad,
):
    qkv_full, attn_out_full, gain_one_bf, bias_full = (
        lax.all_gather(w_qkv, "shard", axis=0, tiled=True),
        lax.all_gather(w_attn_out, "shard", axis=0, tiled=True),
        lax.all_gather(norm1_gain, "shard", axis=0, tiled=True),
        lax.all_gather(b_qkv, "shard", axis=0, tiled=True),
    )
    gate_up_full, down_full, gain_two_bf = (
        lax.all_gather(w_gate_up, "shard", axis=0, tiled=True),
        lax.all_gather(w_down, "shard", axis=0, tiled=True),
        lax.all_gather(norm2_gain, "shard", axis=0, tiled=True),
    )
    tokens = hidden_in.shape[1]
    kv_local = qkv_full.shape[1]
    head_dim = qkv_full.shape[3]
    groups = qkv_full.shape[2] - 2
    query_scale = head_dim ** (-0.5)
    grad_scale = float(lax.axis_size("shard") * lax.axis_size("ctx") * tokens) ** (-0.5)
    gain_one = gain_one_bf.astype(jnp.float32)
    gain_two = gain_two_bf.astype(jnp.float32)
    bias_vals = jnp.transpose(bias_full.astype(jnp.float32), (1, 2, 0))
    inputs = hidden_in[0].astype(jnp.float32)
    seg_row = seg_start[0]
    token_ids = lax.axis_index("ctx") * tokens + jnp.arange(tokens, dtype=jnp.int32)
    cosine, sine_vals = rope_tables((token_ids - seg_row).astype(jnp.float32), head_dim)
    cos_four = cosine[:, None, None, :]
    sin_four = sine_vals[:, None, None, :]
    cos_three = cosine[:, None, :]
    sin_three = sine_vals[:, None, :]
    inv_rms1 = lax.rsqrt(jnp.mean(inputs * inputs, -1, keepdims=True) + EPSILON)
    normed1 = (inputs * inv_rms1 * gain_one).astype(jnp.bfloat16)
    qkv_vals = (
        jnp.einsum("td,dcsh->tcsh", normed1, qkv_full, preferred_element_type=jnp.float32)
        + bias_vals
    )
    q_rot = (apply_rope(qkv_vals[:, :, :groups], cos_four, sin_four) * query_scale).astype(
        jnp.bfloat16
    )
    k_rot = apply_rope(qkv_vals[:, :, groups], cos_three, sin_three).astype(jnp.bfloat16)
    v_vals = qkv_vals[:, :, groups + 1].astype(jnp.bfloat16)
    query_heads = jnp.transpose(q_rot, (1, 2, 0, 3))
    key_value = jnp.stack([k_rot, v_vals], axis=2)

    def allowed_pairs(first_key):
        key_ids = first_key + jnp.arange(tokens, dtype=jnp.int32)
        return (key_ids[None, :] <= token_ids[:, None]) & (key_ids[None, :] >= seg_row[:, None])

    start_state = (
        jnp.full((kv_local, groups, tokens), NEGATIVE, jnp.float32),
        jnp.zeros((kv_local, groups, tokens), jnp.float32),
        jnp.zeros((kv_local, groups, tokens, head_dim), jnp.float32),
    )
    shard_rows = lax.all_gather(key_value, "ctx", axis=0, tiled=True)
    block_count = shard_rows.shape[0] // tokens
    key_blocks = shard_rows.reshape(block_count, tokens, kv_local, 2, head_dim)

    def visit(state, block_pair):
        key_block, block_no = block_pair
        allowed = allowed_pairs(block_no * tokens)

        def update(state_in):
            top_run, total_run, acc_run = state_in
            scores = jnp.einsum(
                "cgqh,kch->cgqk",
                query_heads,
                key_block[:, :, 0],
                preferred_element_type=jnp.float32,
            )
            scores = jnp.where(allowed, scores, NEGATIVE)
            top_new = jnp.maximum(top_run, jnp.max(scores, -1))
            attn_probs = jnp.where(allowed, jnp.exp(scores - top_new[..., None]), 0.0)
            factor = jnp.exp(top_run - top_new)
            total_new = total_run * factor + jnp.sum(attn_probs, -1)
            acc_new = acc_run * factor[..., None] + jnp.einsum(
                "cgqk,kch->cgqh",
                attn_probs,
                key_block[:, :, 1].astype(jnp.float32),
                precision=lax.Precision.HIGHEST,
            )
            return (top_new, total_new, acc_new)

        def keep_state(state_in):
            return state_in

        return (lax.cond(jnp.any(allowed), update, keep_state, state), None)

    final_state, unused = lax.scan(
        visit, start_state, (key_blocks, jnp.arange(block_count, dtype=jnp.int32))
    )
    top_all, total_all, acc_all = final_state
    attn_vals = (acc_all / total_all[..., None]).astype(jnp.bfloat16)
    log_total = top_all + jnp.log(total_all)
    attn_flat = jnp.transpose(attn_vals, (2, 0, 1, 3)).reshape(tokens, kv_local * groups * head_dim)
    resid1 = inputs + tensor_sum(contract_cols(attn_flat, attn_out_full))
    inv_rms2 = lax.rsqrt(jnp.mean(resid1 * resid1, -1, keepdims=True) + EPSILON)
    normed2 = (resid1 * inv_rms2 * gain_two).astype(jnp.bfloat16)
    gate_up = jnp.einsum("td,dsf->tsf", normed2, gate_up_full, preferred_element_type=jnp.float32)
    gate_vals = gate_up[:, 0]
    up_vals = gate_up[:, 1]
    sigmoid_gate = jax.nn.sigmoid(gate_vals)
    silu_gate = gate_vals * sigmoid_gate
    hidden_act = (silu_gate * up_vals).astype(jnp.bfloat16)
    layer_out = resid1 + tensor_sum(contract_cols(hidden_act, down_full))
    grad_rows = out_grad[0]
    d_hidden = jnp.dot(grad_rows, down_full, preferred_element_type=jnp.float32)
    grad_down = contract_rows(grad_rows, hidden_act)
    d_gate = d_hidden * up_vals * sigmoid_gate * (1.0 + gate_vals * (1.0 - sigmoid_gate))
    d_up = d_hidden * silu_gate
    d_gate_up = jnp.stack([d_gate, d_up], 1).astype(jnp.bfloat16)
    grad_gate_up = jnp.einsum("td,tsf->dsf", normed2, d_gate_up, preferred_element_type=jnp.float32)
    d_normed2 = tensor_sum(
        jnp.einsum("tsf,dsf->td", d_gate_up, gate_up_full, preferred_element_type=jnp.float32)
    )
    grad_norm2 = jnp.sum(d_normed2 * resid1 * inv_rms2, 0)
    d_resid1 = grad_rows.astype(jnp.float32) + rms_back(d_normed2, resid1, inv_rms2, gain_two)
    d_resid1_bf = d_resid1.astype(jnp.bfloat16)
    d_attn_flat = jnp.dot(d_resid1_bf, attn_out_full, preferred_element_type=jnp.float32)
    grad_attn_out = contract_rows(d_resid1_bf, attn_flat)
    d_attn = jnp.transpose(d_attn_flat.reshape(tokens, kv_local, groups, head_dim), (1, 2, 0, 3))
    delta_vals = jnp.sum(d_attn * attn_vals.astype(jnp.float32), -1)
    d_attn_bf = d_attn.astype(jnp.bfloat16)
    key_all = lax.all_gather(key_value, "ctx", axis=0, tiled=True)
    block_total = key_all.shape[0] // tokens
    all_blocks = key_all.reshape(block_total, tokens, kv_local, 2, head_dim)

    def revisit(d_query, block_pair):
        key_block, block_no = block_pair
        allowed = allowed_pairs(block_no * tokens)

        def work(d_query_in):
            keys_blk = key_block[:, :, 0]
            values_blk = key_block[:, :, 1]
            scores = jnp.einsum(
                "cgqh,kch->cgqk", query_heads, keys_blk, preferred_element_type=jnp.float32
            )
            attn_probs = jnp.where(allowed, jnp.exp(scores - log_total[..., None]), 0.0)
            probs_bf = attn_probs.astype(jnp.bfloat16)
            d_value = jnp.einsum(
                "cgqk,cgqh->kch", probs_bf, d_attn_bf, preferred_element_type=jnp.float32
            )
            d_probs = jnp.einsum(
                "cgqh,kch->cgqk", d_attn_bf, values_blk, preferred_element_type=jnp.float32
            )
            d_scores = (attn_probs * (d_probs - delta_vals[..., None])).astype(jnp.bfloat16)
            d_query_new = d_query_in + jnp.einsum(
                "cgqk,kch->cgqh", d_scores, keys_blk, preferred_element_type=jnp.float32
            )
            d_key = jnp.einsum(
                "cgqk,cgqh->kch", d_scores, query_heads, preferred_element_type=jnp.float32
            )
            return (d_query_new, jnp.stack([d_key, d_value], 2))

        def skip_block(d_query_in):
            return (d_query_in, jnp.zeros((tokens, kv_local, 2, head_dim), jnp.float32))

        return lax.cond(jnp.any(allowed), work, skip_block, d_query)

    d_query, key_terms = lax.scan(
        revisit,
        jnp.zeros((kv_local, groups, tokens, head_dim), jnp.float32),
        (all_blocks, jnp.arange(block_total, dtype=jnp.int32)),
    )
    key_grads = lax.psum_scatter(
        key_terms.reshape(block_total * tokens, kv_local, 2, head_dim).astype(jnp.bfloat16),
        "ctx",
        scatter_dimension=0,
        tiled=True,
    ).astype(jnp.float32)
    d_query_rows = jnp.transpose(d_query, (2, 0, 1, 3))
    d_qkv = jnp.concatenate(
        [
            rope_grad(d_query_rows, cos_four, sin_four) * query_scale,
            rope_grad(key_grads[:, :, 0], cos_three, sin_three)[:, :, None],
            key_grads[:, :, 1][:, :, None],
        ],
        2,
    )
    grad_bias = jnp.transpose(jnp.sum(d_qkv, 0), (2, 0, 1))
    d_qkv_bf = d_qkv.astype(jnp.bfloat16)
    grad_qkv = jnp.einsum("td,tcsh->dcsh", normed1, d_qkv_bf, preferred_element_type=jnp.float32)
    d_normed1 = tensor_sum(
        jnp.einsum("tcsh,dcsh->td", d_qkv_bf, qkv_full, preferred_element_type=jnp.float32)
    )
    grad_norm1 = jnp.sum(d_normed1 * inputs * inv_rms1, 0)
    in_grad = d_resid1 + rms_back(d_normed1, inputs, inv_rms1, gain_one)
    shares = (
        lax.psum_scatter(
            grad_norm1.astype(jnp.bfloat16), "shard", scatter_dimension=0, tiled=True
        ).astype(jnp.float32),
        lax.psum_scatter(
            grad_qkv.astype(jnp.bfloat16), "shard", scatter_dimension=0, tiled=True
        ).astype(jnp.float32),
        lax.psum_scatter(
            grad_bias.astype(jnp.bfloat16), "shard", scatter_dimension=0, tiled=True
        ).astype(jnp.float32),
        lax.psum_scatter(
            grad_attn_out.astype(jnp.bfloat16), "shard", scatter_dimension=0, tiled=True
        ).astype(jnp.float32),
        lax.psum_scatter(
            grad_norm2.astype(jnp.bfloat16), "shard", scatter_dimension=0, tiled=True
        ).astype(jnp.float32),
        lax.psum_scatter(
            grad_gate_up.astype(jnp.bfloat16), "shard", scatter_dimension=0, tiled=True
        ).astype(jnp.float32),
        lax.psum_scatter(
            grad_down.astype(jnp.bfloat16), "shard", scatter_dimension=0, tiled=True
        ).astype(jnp.float32),
    )
    summed = (
        lax.psum(shares[0].astype(jnp.bfloat16), "ctx").astype(jnp.float32),
        lax.psum(shares[1].astype(jnp.bfloat16), "ctx").astype(jnp.float32),
        lax.psum(shares[2].astype(jnp.bfloat16), "ctx").astype(jnp.float32),
        lax.psum(shares[3].astype(jnp.bfloat16), "ctx").astype(jnp.float32),
        lax.psum(shares[4].astype(jnp.bfloat16), "ctx").astype(jnp.float32),
        lax.psum(shares[5].astype(jnp.bfloat16), "ctx").astype(jnp.float32),
        lax.psum(shares[6].astype(jnp.bfloat16), "ctx").astype(jnp.float32),
    )
    return (
        layer_out[None],
        in_grad[None],
        summed[0] * grad_scale,
        summed[1] * grad_scale,
        summed[2] * grad_scale,
        summed[3] * grad_scale,
        summed[4] * grad_scale,
        summed[5] * grad_scale,
        summed[6] * grad_scale,
    )


def solution(mesh):
    in_specs = (
        P("shard", "ctx", None),
        P("shard", "ctx"),
        P("shard"),
        P("shard", "tp", None, None),
        P("shard", "tp", None),
        P("shard", "tp"),
        P("shard"),
        P("shard", None, "tp"),
        P("shard", "tp"),
        P("shard", "ctx", None),
    )
    out_specs = (
        P("shard", "ctx", None),
        P("shard", "ctx", None),
        P("shard"),
        P("shard", "tp", None, None),
        P("shard", "tp", None),
        P("shard", "tp"),
        P("shard"),
        P("shard", None, "tp"),
        P("shard", "tp"),
    )
    return jax.shard_map(body, mesh=mesh, in_specs=in_specs, out_specs=out_specs, check_vma=False)
```

profile of v0, /device:TPU:0, one launch (start us, length us, event | category | flops | bytes accessed | tf_op | source)
XLA Modules:
  0.0 2073.1 jit_solution(14511887141664644464)
XLA Ops:
  11.6 13.7 all-gather
  26.2 14.1 all_gather.27
  40.4 36.7 %all-gather.7.cloned.1.call-done = bf16[1536,1,8,128]{0,3,2,1:T(8,128)(2,1)} async-done(((bf16[384,1,8,128]{0,3,2,1:T(8,128)(2,1)}), bf16[1536,1,8,128]{0,3,2,1:T(8,128)(2,1)}) %all-gather.7.cloned.1.call-update) | async-done | bytes 3145744 | tf_op jit(solution)/shard_map/all_gather | solution.py:74
  90.0 11.6 while.31
  101.8 25.5 %all-gather.9.cloned.1.call-done = bf16[1536,768]{1,0:T(8,128)(2,1)} async-done(((bf16[384,768]{1,0:T(8,128)(2,1)}), bf16[1536,768]{1,0:T(8,128)(2,1)}) %all-gather.9.cloned.1.call-update) | async-done | bytes 2359312 | tf_op jit(solution)/shard_map/all_gather | solution.py:75
  138.2 12.1 all-gather.1
  151.7 463.0 %all-gather.11.cloned.1.call-done = bf16[1536,2,4480]{2,0,1:T(8,128)(2,1)} async-done(((bf16[384,2,4480]{2,0,1:T(8,128)(2,1)}), bf16[1536,2,4480]{2,0,1:T(8,128)(2,1)}) %all-gather.11.cloned.1.call-update) | async-done | bytes 27525136 | tf_op jit(solution)/shard_map/all_gather | solution.py:80
  614.7 16.3 fusion.96
  631.1 220.8 %all-gather.13.cloned.1.call-done = bf16[1536,4480]{1,0:T(8,128)(2,1)} async-done(((bf16[384,4480]{1,0:T(8,128)(2,1)}), bf16[1536,4480]{1,0:T(8,128)(2,1)}) %all-gather.13.cloned.1.call-update) | async-done | bytes 13762576 | tf_op jit(solution)/shard_map/all_gather | solution.py:81
  862.1 15.3 convolution_bitcast_fusion.5
  878.1 16.7 all-reduce.13.cloned.1.call-done
  899.7 17.8 while.32
  931.1 18.5 copy.99
  957.7 14.5 convolution_convert_fusion
  972.5 11.8 fusion.43
  988.7 195.9 %reduce-scatter.23.cloned.1.call-done = bf16[384,4480]{1,0:T(8,128)(2,1)} async-done(((bf16[1536,4480]{1,0:T(8,128)(2,1)}), bf16[384,4480]{1,0:T(8,128)(2,1)}) %reduce-scatter.23.cloned.1.call-update) | async-done | bytes 3440656
  1190.5 45.2 %reduce-scatter.15.cloned.1.call-done = bf16[384,768]{1,0:T(8,128)(2,1)} async-done(((bf16[1536,768]{1,0:T(8,128)(2,1)}), bf16[384,768]{1,0:T(8,128)(2,1)}) %reduce-scatter.15.cloned.1.call-update) | async-done | bytes 589840 | tf_op jit(solution)/shard_map/reduce_scatter | solution.py:267
  1235.7 62.5 %reduce-scatter.13.cloned.1.call-done = bf16[384,1,8,128]{3,0,2,1:T(8,128)(2,1)} async-done(((bf16[1536,1,8,128]{3,0,2,1:T(8,128)(2,1)}), bf16[384,1,8,128]{3,0,2,1:T(8,128)(2,1)}) %reduce-scatter.13.cloned.1.call-update) | async-done | bytes 786448 | tf_op jit(solution)/shard_map/reduce_scatter | solution.py:261
  1298.3 454.4 %reduce-scatter.17.cloned.1.call-done = bf16[384,2,4480]{2,0,1:T(8,128)(2,1)} async-done(((bf16[1536,2,4480]{2,0,1:T(8,128)(2,1)}), bf16[384,2,4480]{2,0,1:T(8,128)(2,1)}) %reduce-scatter.17.cloned.1.call-update) | async-done | bytes 6881296 | tf_op jit(solution)/shard_map/reduce_scatter | solution.py:273
  1754.6 22.1 %reduce-scatter.21.cloned.1.call-done = bf16[32,8]{1,0:T(8,128)(2,1)} async-done(((bf16[128,8]{1,0:T(8,128)(2,1)}), bf16[32,8]{1,0:T(8,128)(2,1)}) %reduce-scatter.21.cloned.1.call-update) | async-done | bytes 528
  1777.5 20.8 %all-reduce.15.cloned.1.call-done = (f32[128,1536]{1,0:T(8,128)}, f32[128,1536]{1,0:T(8,128)}) async-done(((f32[128,1536]{1,0:T(8,128)}, f32[128,1536]{1,0:T(8,128)}), (f32[128,1536]{1,0:T(8,128)}, f32[128,1536]{1,0:T(8,128)})) %all-reduce.15.cloned.1.call-update) | async-done | bytes 1572880 | tf_op jit(solution)/shard_map/psum | solution.py:46
  1799.7 12.1 all-reduce.5
  1827.5 202.5 %all-reduce.17.cloned.1.call-done = (bf16[384,1,8,128]{3,0,2,1:T(8,128)(2,1)}, bf16[384,768]{1,0:T(8,128)(2,1)}, bf16[384,2,4480]{2,0,1:T(8,128)(2,1)}, bf16[384,4480]{0,1:T(8,128)(2,1)}) async-done(((bf16[384,1,8,128]{3,0,2,1:T(8,128)(2,1)}, bf16[384,768]{1,0:T(8,128)(2,1)}, bf16[384,2,4480]{2,0,1:T(8,128)(2,1)}, bf16[384,4480]{0,1:T(8,128)(2,1)}), (bf16[384,1,8,128]{3,0,2,1:T(8,128)(2,1)}, ...) | async-done | bytes 11698192 | tf_op jit(solution)/shard_map/psum | solution.py:282
  2038.7 15.6 copy.83
  (223 shorter events, 139.5 us)
Async XLA Ops:
  7.2 69.9 %all-gather.7.cloned.1.call-start = ((), (), s32[]{:S(2)}) async-start(), calls=%async_computation.6 | async-start | bytes 3932160 | tf_op jit(solution)/shard_map/all_gather | solution.py:74
  9.8 117.6 %all-gather.9.cloned.1.call-start = ((), (), s32[]{:S(2)}) async-start(), calls=%async_computation.7 | async-start | bytes 2949120 | tf_op jit(solution)/shard_map/all_gather | solution.py:75
  10.5 139.8 %all-reduce.11.cloned.1.call-start = ((), (), s32[]{:S(2)}) async-start(), calls=%async_computation.8 | async-start | bytes 1572864 | tf_op jit(solution)/shard_map/psum | solution.py:46
  10.8 69.6 %copy-start.8 = (f32[128,1,1,64]{0,3,2,1:T(8,128)}, f32[128,1,1,64]{0,3,2,1:T(8,128)S(1)}, u32[]{:S(2)}) copy-start(f32[128,1,1,64]{0,3,2,1:T(8,128)S(1)} %multiply_cosine_fusion.1) | copy-start | bytes 98308
  26.0 54.3 %copy-start.18 = (f32[128]{0:T(128)}, f32[128]{0:T(128)S(1)}, u32[]{:S(2)}) copy-start(f32[128]{0:T(128)S(1)} %get-tuple-element.441) | copy-start | bytes 1540
  26.1 54.2 %copy-start.10 = (f32[1536]{0:T(1024)}, f32[1536]{0:T(1024)S(1)}, u32[]{:S(2)}) copy-start(f32[1536]{0:T(1024)S(1)} %reshape.542) | copy-start | bytes 18436
  101.8 35.6 %copy-start.4 = (bf16[1,6,128,128]{2,3,1,0:T(8,128)(2,1)}, bf16[1,6,128,128]{2,3,1,0:T(8,128)(2,1)S(1)}, u32[]{:S(2)}) copy-start(bf16[1,6,128,128]{2,3,1,0:T(8,128)(2,1)S(1)} %divide_convert_fusion) | copy-start | bytes 589828
  130.8 483.9 %all-gather.11.cloned.1.call-start = ((), (), s32[]{:S(2)}) async-start(), calls=%async_computation.9 | async-start | bytes 34406400 | tf_op jit(solution)/shard_map/all_gather | solution.py:80
  137.5 714.3 %all-gather.13.cloned.1.call-start = ((), (), s32[]{:S(2)}) async-start(), calls=%async_computation.10 | async-start | bytes 17203200 | tf_op jit(solution)/shard_map/all_gather | solution.py:81
  138.1 756.7 %all-reduce.13.cloned.1.call-start = ((), (), s32[]{:S(2)}) async-start(), calls=%async_computation.11 | async-start | bytes 1572864 | tf_op jit(solution)/shard_map/psum | solution.py:46
  151.7 745.2 %copy-start.15 = (f32[128]{0:T(128)}, f32[128]{0:T(128)S(1)}, u32[]{:S(2)}) copy-start(f32[128]{0:T(128)S(1)} %get-tuple-element.443) | copy-start | bytes 1540
  614.7 237.1 %copy-start.6 = (bf16[1,128,1536]{2,1,0:T(8,128)(2,1)S(1)}, bf16[1,128,1536]{2,1,0:T(8,128)(2,1)}, u32[]{:S(2)}) copy-start(bf16[1,128,1536]{2,1,0:T(8,128)(2,1)} %param.27) | copy-start | bytes 1179652
  877.4 75.7 %reduce-scatter.19.cloned.1.call-start = ((), (), s32[]{:S(2)}) async-start(), calls=%async_computation.15 | async-start | bytes 327680
  919.5 265.1 %reduce-scatter.23.cloned.1.call-start = ((), (), s32[]{:S(2)}) async-start(), calls=%async_computation.17 | async-start | bytes 17203200
  949.6 286.1 %reduce-scatter.15.cloned.1.call-start = ((), (), s32[]{:S(2)}) async-start(), calls=%async_computation.13 | async-start | bytes 2949120 | tf_op jit(solution)/shard_map/reduce_scatter | solution.py:267
  952.8 345.5 %reduce-scatter.13.cloned.1.call-start = ((), (), s32[]{:S(2)}) async-start(), calls=%async_computation.12 | async-start | bytes 3932160 | tf_op jit(solution)/shard_map/reduce_scatter | solution.py:261
  957.1 795.6 %reduce-scatter.17.cloned.1.call-start = ((), (), s32[]{:S(2)}) async-start(), calls=%async_computation.14 | async-start | bytes 34406400 | tf_op jit(solution)/shard_map/reduce_scatter | solution.py:273
  972.2 804.5 %reduce-scatter.21.cloned.1.call-start = ((), (), s32[]{:S(2)}) async-start(), calls=%async_computation.16 | async-start | bytes 40960
  985.2 813.1 %all-reduce.15.cloned.1.call-start = ((), (), s32[]{:S(2)}) async-start(), calls=%async_computation.18 | async-start | bytes 3145728 | tf_op jit(solution)/shard_map/psum | solution.py:46
  988.7 1041.3 %all-reduce.17.cloned.1.call-start = ((), (), s32[]{:S(2)}) async-start(), calls=%async_computation.19 | async-start | bytes 23396352 | tf_op jit(solution)/shard_map/psum | solution.py:282
  1752.7 45.6 %copy-start.12 = (f32[1536]{0:T(1024)S(1)}, f32[1536]{0:T(1024)}, u32[]{:S(2)}) copy-start(f32[1536]{0:T(1024)} %copy-done.10) | copy-start | bytes 18436
  1752.7 47.0 %copy-start.17 = (bf16[1536]{0:T(1024)(128)(2,1)S(1)}, bf16[1536]{0:T(1024)(128)(2,1)}, u32[]{:S(2)}) copy-start(bf16[1536]{0:T(1024)(128)(2,1)} %get-tuple-element.353) | copy-start | bytes 9220
  1752.7 73.6 %copy-start.23 = (f32[128]{0:T(128)S(1)}, f32[128]{0:T(128)}, u32[]{:S(2)}) copy-start(f32[128]{0:T(128)} %get-tuple-element.440) | copy-start | bytes 1540
  1798.3 28.0 %copy-start.3 = (f32[128,1536]{1,0:T(8,128)S(1)}, f32[128,1536]{1,0:T(8,128)}, u32[]{:S(2)}) copy-start(f32[128,1536]{1,0:T(8,128)} %get-tuple-element.398) | copy-start | bytes 2359300
  (15 other events, 76.0 us)
Sparse Core Ops, SparseCore 0:
  10.2 66.9 all-gather.6
  78.7 48.6 all-gather.8
  130.9 17.7 all-reduce.10
  150.7 463.9 all-gather.10
  616.1 235.6 all-gather.12
  877.6 17.1 all-reduce.12
  919.6 28.2 reduce-scatter.18
  950.3 234.2 reduce-scatter.22
  1186.9 48.7 reduce-scatter.14
  1238.5 59.7 reduce-scatter.12
  1300.6 452.0 reduce-scatter.16
  1755.4 21.2 reduce-scatter.20
  1779.6 18.6 all-reduce.14
  1802.7 227.2 all-reduce.16
where the time goes:
time: 2080 us; the launch traced here: 2070 us
  waiting for transfers between devices  1770 us (85%)
  matrix products  97.9 us (5%)
  local copies, waits for them, and re-layouts  75.4 us (4%)
  blocking collectives  71.3 us (3%)
  other arithmetic  33.4 us (2%)
    all_gather x1, waiting for transfers between devices, body(): lax.all_gather(w_gate_up, 'shard', axis=0, tiled=True)  463 us
    reduce_scatter x1, waiting for transfers between devices, body(): lax.psum_scatter(grad_gate_up.astype(jnp.bfloat16), 'shard', scatter_dime...  454 us
    all_gather x1, waiting for transfers between devices, body(): lax.all_gather(w_down, 'shard', axis=0, tiled=True)  221 us
    unnamed x17, waiting for transfers between devices  219 us
    psum x1, waiting for transfers between devices, body(): lax.psum(shares[1].astype(jnp.bfloat16), 'ctx').astype(jnp.float32)  202 us
    unnamed x71, local copies, waits for them, and re-layouts  67.4 us
    reduce_scatter x1, waiting for transfers between devices, body(): lax.psum_scatter(grad_qkv.astype(jnp.bfloat16), 'shard', scatter_dimensio...  62.5 us
    reduce_scatter x1, waiting for transfers between devices, body(): lax.psum_scatter(grad_attn_out.astype(jnp.bfloat16), 'shard', scatter_dim...  45.2 us
  transfers between devices with their start and end apart: 14, of which 12 were waited for; matrix products, arithmetic and copies ran while one was open for 6% of the time, Pallas kernels for 0%

commit v1 on v0

v1 whole, which is shorter than its diff:
```python
import jax
import jax.numpy as jnp
from jax import lax
from jax.sharding import PartitionSpec as P

EPSILON = 1e-06
ROPE_BASE = 1000000.0
NEGATIVE = -1e30


def rope_tables(positions, head_dim):
    half_dim = head_dim // 2
    frequency = ROPE_BASE ** (-(jnp.arange(half_dim, dtype=jnp.float32) * 2.0) / head_dim)
    angles = positions[:, None] * frequency[None, :]
    cosine = jnp.cos(angles)
    sine_vals = jnp.sin(angles)
    return (jnp.concatenate([cosine, cosine], -1), jnp.concatenate([sine_vals, sine_vals], -1))


def rotate_half(values):
    half_dim = values.shape[-1] // 2
    return jnp.concatenate([-values[..., half_dim:], values[..., :half_dim]], -1)


def rotate_back(values):
    half_dim = values.shape[-1] // 2
    return jnp.concatenate([values[..., half_dim:], -values[..., :half_dim]], -1)


def apply_rope(values, cosine, sine_vals):
    return values * cosine + rotate_half(values) * sine_vals


def rope_grad(grads, cosine, sine_vals):
    return grads * cosine + rotate_back(grads * sine_vals)


def rms_back(grad_norm, inputs, inv_rms, gain_vals):
    scaled = gain_vals * grad_norm
    return inv_rms * scaled - inputs * (inv_rms * inv_rms * inv_rms) * jnp.mean(
        scaled * inputs, -1, keepdims=True
    )


def tensor_sum(partial_sum):
    return lax.psum(partial_sum, "tp")


def contract_rows(left, right):
    return lax.dot_general(
        left, right, (((0,), (0,)), ((), ())), preferred_element_type=jnp.float32
    )


def contract_cols(left, right):
    return lax.dot_general(
        left, right, (((1,), (1,)), ((), ())), preferred_element_type=jnp.float32
    )

def body(
    hidden_in,
    seg_start,
    norm1_gain,
    w_qkv,
    b_qkv,
    w_attn_out,
    norm2_gain,
    w_gate_up,
    w_down,
    out_grad,
):
    shards = lax.axis_size("shard")
    ctxs = lax.axis_size("ctx")
    ctx_id = lax.axis_index("ctx")
    tp_id = lax.axis_index("tp")
    everyone = ("shard", "ctx", "tp")
    bf16 = jnp.bfloat16
    qkv_full, attn_out_full, gain_one_bf, bias_full, gain_two_bf = (
        lax.all_gather(w_qkv, "shard", axis=0, tiled=True),
        lax.all_gather(w_attn_out, "shard", axis=0, tiled=True),
        lax.all_gather(norm1_gain, "shard", axis=0, tiled=True),
        lax.all_gather(b_qkv, "shard", axis=0, tiled=True),
        lax.all_gather(norm2_gain, "shard", axis=0, tiled=True),
    )
    tokens, width = hidden_in.shape[1], hidden_in.shape[2]
    half = tokens // lax.axis_size("tp")
    part = w_gate_up.shape[0]
    hidden_units = w_down.shape[1] // (shards * ctxs)

    def my_units(weights):
        blocks = weights.reshape(weights.shape[:-1] + (ctxs, shards * hidden_units))
        return lax.dynamic_index_in_dim(blocks, ctx_id, weights.ndim - 1, keepdims=False)

    def my_half(rows):
        return lax.dynamic_slice_in_dim(rows, tp_id * half, half, 0)

    mine = jnp.concatenate([my_units(w_gate_up), my_units(w_down)[:, None]], 1)
    mine = jnp.transpose(mine.reshape(part, 3, shards, hidden_units), (2, 0, 1, 3))
    units = lax.all_to_all(mine, "shard", split_axis=0, concat_axis=0, tiled=True)
    units = units.reshape(shards * part, 3, hidden_units)
    gate_up_w = units[:, :2].reshape(shards * part, 2 * hidden_units)
    down_w = units[:, 2]
    grad_rows = out_grad[0]
    grad_all = lax.all_gather(my_half(grad_rows), everyone, axis=0, tiled=True)

    kv_local = qkv_full.shape[1]
    head_dim = qkv_full.shape[3]
    groups = qkv_full.shape[2] - 2
    query_scale = head_dim ** (-0.5)
    grad_scale = float(shards * ctxs * tokens) ** (-0.5)
    gain_one = gain_one_bf.astype(jnp.float32)
    gain_two = gain_two_bf.astype(jnp.float32)
    bias_vals = jnp.transpose(bias_full.astype(jnp.float32), (1, 2, 0))
    inputs = hidden_in[0].astype(jnp.float32)
    seg_row = seg_start[0]
    token_ids = ctx_id * tokens + jnp.arange(tokens, dtype=jnp.int32)
    cosine, sine_vals = rope_tables((token_ids - seg_row).astype(jnp.float32), head_dim)
    cos_four = cosine[:, None, None, :]
    sin_four = sine_vals[:, None, None, :]
    cos_three = cosine[:, None, :]
    sin_three = sine_vals[:, None, :]
    inv_rms1 = lax.rsqrt(jnp.mean(inputs * inputs, -1, keepdims=True) + EPSILON)
    normed1 = (inputs * inv_rms1 * gain_one).astype(bf16)
    qkv_vals = (
        jnp.einsum("td,dcsh->tcsh", normed1, qkv_full, preferred_element_type=jnp.float32)
        + bias_vals
    )
    q_rot = (apply_rope(qkv_vals[:, :, :groups], cos_four, sin_four) * query_scale).astype(bf16)
    k_rot = apply_rope(qkv_vals[:, :, groups], cos_three, sin_three).astype(bf16)
    v_vals = qkv_vals[:, :, groups + 1].astype(bf16)
    query_heads = jnp.transpose(q_rot, (1, 2, 0, 3))
    key_value = jnp.stack([k_rot, v_vals], axis=2)
    key_value = lax.all_gather(key_value, "ctx", axis=0, tiled=True)
    keys, values = key_value[:, :, 0], key_value[:, :, 1]
    length = keys.shape[0]
    key_ids = jnp.arange(length, dtype=jnp.int32)
    allowed = (key_ids[None, :] <= token_ids[:, None]) & (key_ids[None, :] >= seg_row[:, None])
    scores = jnp.einsum("cgqh,kch->cgqk", query_heads, keys, preferred_element_type=jnp.float32)
    scores = jnp.where(allowed, scores, NEGATIVE)
    top_all = jnp.max(scores, -1, keepdims=True)
    raised = jnp.where(allowed, jnp.exp(scores - top_all), 0.0)
    total_all = jnp.sum(raised, -1, keepdims=True)
    attn_probs = raised / total_all
    probs_bf = attn_probs.astype(bf16)
    attn_vals = jnp.einsum(
        "cgqk,kch->cgqh", probs_bf, values, preferred_element_type=jnp.float32
    ).astype(bf16)
    attn_flat = jnp.transpose(attn_vals, (2, 0, 1, 3)).reshape(tokens, kv_local * groups * head_dim)
    resid1 = inputs + tensor_sum(contract_cols(attn_flat, attn_out_full))
    inv_rms2 = lax.rsqrt(jnp.mean(resid1 * resid1, -1, keepdims=True) + EPSILON)
    normed2 = (resid1 * inv_rms2 * gain_two).astype(bf16)

    normed2_all = lax.all_gather(my_half(normed2), everyone, axis=0, tiled=True)
    gate_up = jnp.dot(normed2_all, gate_up_w, preferred_element_type=jnp.float32)
    gate_vals, up_vals = gate_up[:, :hidden_units], gate_up[:, hidden_units:]
    sigmoid_gate = jax.nn.sigmoid(gate_vals)
    silu_gate = gate_vals * sigmoid_gate
    hidden_act = (silu_gate * up_vals).astype(bf16)
    d_hidden = jnp.dot(grad_all, down_w, preferred_element_type=jnp.float32)
    d_gate = d_hidden * up_vals * sigmoid_gate * (1.0 + gate_vals * (1.0 - sigmoid_gate))
    d_up = d_hidden * silu_gate
    d_gate_up = jnp.concatenate([d_gate, d_up], 1).astype(bf16)

    def scatter_sum(partial_sum):
        share = lax.psum_scatter(
            partial_sum.astype(bf16), everyone, scatter_dimension=0, tiled=True
        )
        return lax.all_gather(share, "tp", axis=0, tiled=True).astype(jnp.float32)

    d_normed2 = scatter_sum(contract_cols(d_gate_up, gate_up_w))
    layer_out = resid1 + scatter_sum(contract_cols(hidden_act, down_w))
    grad_down = contract_rows(grad_all, hidden_act).astype(bf16)
    grad_gate_up = contract_rows(normed2_all, d_gate_up).astype(bf16)
    made = jnp.concatenate([grad_gate_up, grad_down], 1).reshape(shards, part, 3 * hidden_units)
    made = lax.all_to_all(made, "shard", split_axis=0, concat_axis=0, tiled=True)
    made = lax.all_gather(made, "ctx", axis=0, tiled=False)
    made = made.reshape(ctxs, shards, part, 3, hidden_units)
    made = jnp.transpose(made, (2, 3, 0, 1, 4)).reshape(part, 3, ctxs * shards * hidden_units)
    made = made.astype(jnp.float32) * grad_scale

    grad_norm2 = jnp.sum(d_normed2 * resid1 * inv_rms2, 0)
    d_resid1 = grad_rows.astype(jnp.float32) + rms_back(d_normed2, resid1, inv_rms2, gain_two)
    d_resid1_bf = d_resid1.astype(bf16)
    d_attn_flat = jnp.dot(d_resid1_bf, attn_out_full, preferred_element_type=jnp.float32)
    grad_attn_out = contract_rows(d_resid1_bf, attn_flat)
    d_attn = jnp.transpose(d_attn_flat.reshape(tokens, kv_local, groups, head_dim), (1, 2, 0, 3))
    delta_vals = jnp.sum(d_attn * attn_vals.astype(jnp.float32), -1)
    d_attn_bf = d_attn.astype(bf16)
    d_value = jnp.einsum("cgqk,cgqh->kch", probs_bf, d_attn_bf, preferred_element_type=jnp.float32)
    d_probs = jnp.einsum("cgqh,kch->cgqk", d_attn_bf, values, preferred_element_type=jnp.float32)
    d_scores = (attn_probs * (d_probs - delta_vals[..., None])).astype(bf16)
    d_query = jnp.einsum("cgqk,kch->cgqh", d_scores, keys, preferred_element_type=jnp.float32)
    d_key = jnp.einsum("cgqk,cgqh->kch", d_scores, query_heads, preferred_element_type=jnp.float32)
    key_grads = lax.psum_scatter(
        jnp.stack([d_key, d_value], 2).astype(bf16), "ctx", scatter_dimension=0, tiled=True
    ).astype(jnp.float32)
    d_query_rows = jnp.transpose(d_query, (2, 0, 1, 3))
    d_qkv = jnp.concatenate(
        [
            rope_grad(d_query_rows, cos_four, sin_four) * query_scale,
            rope_grad(key_grads[:, :, 0], cos_three, sin_three)[:, :, None],
            key_grads[:, :, 1][:, :, None],
        ],
        2,
    )
    grad_bias = jnp.transpose(jnp.sum(d_qkv, 0), (2, 0, 1))
    d_qkv_bf = d_qkv.astype(bf16)
    grad_qkv = jnp.einsum("td,tcsh->dcsh", normed1, d_qkv_bf, preferred_element_type=jnp.float32)
    d_normed1 = tensor_sum(
        jnp.einsum("tcsh,dcsh->td", d_qkv_bf, qkv_full, preferred_element_type=jnp.float32)
    )
    grad_norm1 = jnp.sum(d_normed1 * inputs * inv_rms1, 0)
    in_grad = d_resid1 + rms_back(d_normed1, inputs, inv_rms1, gain_one)

    def total(partial_sum):
        share = lax.psum_scatter(
            partial_sum.astype(bf16), "shard", scatter_dimension=0, tiled=True
        )
        return lax.psum(share, "ctx").astype(jnp.float32) * grad_scale

    return (
        layer_out[None],
        in_grad[None],
        total(grad_norm1),
        total(grad_qkv),
        total(grad_bias),
        total(grad_attn_out),
        total(grad_norm2),
        made[:, :2],
        made[:, 2],
    )


def solution(mesh):
    in_specs = (
        P("shard", "ctx", None),
        P("shard", "ctx"),
        P("shard"),
        P("shard", "tp", None, None),
        P("shard", "tp", None),
        P("shard", "tp"),
        P("shard"),
        P("shard", None, "tp"),
        P("shard", "tp"),
        P("shard", "ctx", None),
    )
    out_specs = (
        P("shard", "ctx", None),
        P("shard", "ctx", None),
        P("shard"),
        P("shard", "tp", None, None),
        P("shard", "tp", None),
        P("shard", "tp"),
        P("shard"),
        P("shard", None, "tp"),
        P("shard", "tp"),
    )
    return jax.shard_map(body, mesh=mesh, in_specs=in_specs, out_specs=out_specs, check_vma=False)
```

time: 2080 us -> 1050 us (0.50)
  waiting for transfers between devices: 1770 us -> 663 us
  blocking collectives: 71.3 us -> 162 us
  matrix products: 97.9 us -> 63.1 us
  local copies, waits for them, and re-layouts: 75.4 us -> 105 us
    all_gather x2 -> x3, waiting for transfers between devices: 684 us -> 144 us  [the longest x1 101 us: body(): made = lax.all_gather(made, 'ctx', axis=0, tiled=False)]
    reduce_scatter x3 -> x4, waiting for transfers between devices: 562 us -> 348 us  [the longest x2 222 us: scatter_sum(): lax.psum_scatter(partial_sum.astype(bf16), everyone, scatter_dimension=0,...]
    unnamed x17 -> x16, waiting for transfers between devices: 219 us -> 40.1 us
    psum x1, waiting for transfers between devices: 202 us -> 34.2 us  [total(): return lax.psum(share, 'ctx').astype(jnp.float32) * grad_scale]
    all_to_all x0 -> x1, blocking collectives: none -> 85.7 us  [body(): lax.all_to_all(mine, 'shard', split_axis=0, concat_axis=0, tiled=True)]
    dot_general x11 -> x7, matrix products: 59 us -> 18.9 us  [the longest x1 9.18 us: body(): jnp.dot(normed2_all, gate_up_w, preferred_element_type=jnp.float32)]
    unnamed x71 -> x98, local copies, waits for them, and re-layouts: 67.4 us -> 74.5 us
  transfers between devices with their start and end apart: 14 -> 15, of which waited for: 12 -> 13; matrix products, arithmetic and copies ran while one was open for 6% -> 9% of each run, Pallas kernels for 0% -> 0%
where the time goes in v1:
time: 1050 us
  waiting for transfers between devices  663 us (63%)
  blocking collectives  162 us (15%)
  local copies, waits for them, and re-layouts  105 us (10%)
  matrix products  63.1 us (6%)
  other arithmetic  32.7 us (3%)
  between operations  15.3 us (1%)
    reduce_scatter x2, waiting for transfers between devices, scatter_sum(): lax.psum_scatter(partial_sum.astype(bf16), everyone, scatter_dimension=0,...  222 us
    reduce_scatter x2, waiting for transfers between devices, total(): lax.psum_scatter(partial_sum.astype(bf16), 'shard', scatter_dimension=0,...  126 us
    all_gather x1, waiting for transfers between devices, body(): made = lax.all_gather(made, 'ctx', axis=0, tiled=False)  101 us
    all_to_all x1, blocking collectives, body(): lax.all_to_all(mine, 'shard', split_axis=0, concat_axis=0, tiled=True)  85.7 us
    unnamed x98, local copies, waits for them, and re-layouts  74.5 us
    all_gather x1, waiting for transfers between devices, body(): grad_all = lax.all_gather(my_half(grad_rows), everyone, axis=0, tiled=True)  42.8 us
    unnamed x16, waiting for transfers between devices  40.1 us
    all_gather x1, waiting for transfers between devices, body(): lax.all_gather(w_attn_out, 'shard', axis=0, tiled=True)  36.5 us
  transfers between devices with their start and end apart: 15, of which 13 were waited for; matrix products, arithmetic and copies ran while one was open for 9% of the time, Pallas kernels for 0%

profile of v1, /device:TPU:0, one launch (start us, length us, event | category | flops | bytes accessed | tf_op | source)
XLA Modules:
  0.0 1046.7 jit_solution(12587943593719788081)
XLA Ops:
  10.6 13.6 %all-gather.2 = bf16[4,1,384]{2,1,0:T(2,128)(2,1)S(1)} all-gather(bf16[1,1,384]{2,1,0:T(2,128)(2,1)S(1)} %reshape.562), channel_id=1, replica_groups=mesh['shard'=4,'ctx'=4,'tp'=2] {'shard'}, dimensions={0}, use_global_device_ids=true | all-gather | bytes 3840 | tf_op jit(solution)/shard_map/all_gather | solution.py:81
  25.2 15.2 %all_gather.38 = bf16[128,1,8]{2,1,0:T(2,128)(2,1)S(1)} all-gather(bf16[32,1,8]{2,1,0:T(2,128)(2,1)S(1)} %copy.68), channel_id=1, replica_groups=mesh['shard'=4,'ctx'=4,'tp'=2] {'shard'}, dimensions={0}, use_global_device_ids=true | all-gather | bytes 2560 | tf_op jit(solution)/shard_map/all_gather | solution.py:82
  41.7 35.5 %all-gather.10.cloned.1.call-done = bf16[1536,1,8,128]{0,3,2,1:T(8,128)(2,1)} async-done(((bf16[384,1,8,128]{0,3,2,1:T(8,128)(2,1)}), bf16[1536,1,8,128]{0,3,2,1:T(8,128)(2,1)}) %all-gather.10.cloned.1.call-update) | async-done | bytes 3145744 | tf_op jit(solution)/shard_map/all_gather | solution.py:79
  80.4 8.9 all_gather.39
  90.9 36.5 %all-gather.12.cloned.1.call-done = bf16[1536,768]{1,0:T(8,128)(2,1)} async-done(((bf16[384,768]{1,0:T(8,128)(2,1)}), bf16[1536,768]{1,0:T(8,128)(2,1)}) %all-gather.12.cloned.1.call-update) | async-done | bytes 2359312 | tf_op jit(solution)/shard_map/all_gather | solution.py:80
  130.9 12.1 %all-gather.3 = bf16[4,1,384]{2,1,0:T(2,128)(2,1)S(1)} all-gather(bf16[1,1,384]{2,1,0:T(2,128)(2,1)S(1)} %reshape.564), channel_id=1, replica_groups=mesh['shard'=4,'ctx'=4,'tp'=2] {'shard'}, dimensions={0}, use_global_device_ids=true | all-gather | bytes 3840 | tf_op jit(solution)/shard_map/all_gather | solution.py:83
  158.1 18.0 %copy.72 = bf16[384,2,4480]{0,2,1:T(8,128)(2,1)} copy(bf16[384,2,4480]{2,1,0:T(2,128)(2,1)} %param.17) | data formatting | bytes 13762560 | tf_op args[7]
  179.6 85.7 %all_to_all.10 = bf16[4,384,3,280]{1,3,2,0:T(8,128)(2,1)S(1)} all-to-all(bf16[4,384,3,280]{1,3,2,0:T(8,128)(2,1)S(1)} %copy.74), channel_id=1, replica_groups=mesh['shard'=4,'ctx'=4,'tp'=2] {'shard'}, dimensions={0} | all-to-all | bytes 5160960 | tf_op jit(solution)/shard_map/all_to_all | solution.py:99
  268.4 9.2 fusion.91
  277.5 42.8 %all-gather.16.cloned.1.call-done = bf16[1,2048,1536]{2,1,0:T(8,128)(2,1)} async-done(((bf16[1,64,1536]{2,1,0:T(8,128)(2,1)}), bf16[1,2048,1536]{2,1,0:T(8,128)(2,1)}) %all-gather.16.cloned.1.call-update) | async-done | bytes 6291472 | tf_op jit(solution)/shard_map/all_gather | solution.py:104
  344.7 105.9 %reduce-scatter.13.cloned.1.call-done = bf16[64,1536]{1,0:T(8,128)(2,1)} async-done(((bf16[2048,1536]{1,0:T(8,128)(2,1)}), bf16[64,1536]{1,0:T(8,128)(2,1)}) %reduce-scatter.13.cloned.1.call-update) | async-done | bytes 196624 | tf_op jit(solution)/shard_map/reduce_scatter | solution.py:165
  454.2 116.5 %reduce-scatter.11.cloned.1.call-done = bf16[64,1536]{1,0:T(8,128)(2,1)} async-done(((bf16[2048,1536]{1,0:T(8,128)(2,1)}), bf16[64,1536]{1,0:T(8,128)(2,1)}) %reduce-scatter.11.cloned.1.call-update) | async-done | bytes 196624 | tf_op jit(solution)/shard_map/reduce_scatter | solution.py:165
  584.5 19.4 %reduce-scatter.19.cloned.1.call-done = bf16[128,256]{1,0:T(8,128)(2,1)} async-done(((bf16[512,256]{1,0:T(8,128)(2,1)}), bf16[128,256]{1,0:T(8,128)(2,1)}) %reduce-scatter.19.cloned.1.call-update) | async-done | bytes 65552
  634.2 43.2 %reduce-scatter.17.cloned.1.call-done = bf16[384,768]{1,0:T(8,128)(2,1)} async-done(((bf16[1536,768]{1,0:T(8,128)(2,1)}), bf16[384,768]{1,0:T(8,128)(2,1)}) %reduce-scatter.17.cloned.1.call-update) | async-done | bytes 589840 | tf_op jit(solution)/shard_map/reduce_scatter | solution.py:216
  677.4 82.8 %reduce-scatter.15.cloned.1.call-done = bf16[384,1,8,128]{3,0,2,1:T(8,128)(2,1)} async-done(((bf16[1536,1,8,128]{3,0,2,1:T(8,128)(2,1)}), bf16[384,1,8,128]{3,0,2,1:T(8,128)(2,1)}) %reduce-scatter.15.cloned.1.call-update) | async-done | bytes 786448 | tf_op jit(solution)/shard_map/reduce_scatter | solution.py:216
  762.0 19.3 %reduce-scatter.21.cloned.1.call-done = bf16[32,8]{1,0:T(8,128)(2,1)} async-done(((bf16[128,8]{1,0:T(8,128)(2,1)}), bf16[32,8]{1,0:T(8,128)(2,1)}) %reduce-scatter.21.cloned.1.call-update) | async-done | bytes 528
  782.1 19.1 %all-reduce.11.cloned.1.call-done = f32[128,1536]{1,0:T(8,128)} async-done(((f32[128,1536]{1,0:T(8,128)}), f32[128,1536]{1,0:T(8,128)}) %all-reduce.11.cloned.1.call-update) | async-done | bytes 786448 | tf_op jit(solution)/shard_map/psum | solution.py:46
  802.6 12.2 %all-reduce.4 = (bf16[1536]{0:T(1024)(128)(2,1)S(1)}, bf16[1536]{0:T(1024)(128)(2,1)S(1)}) all-reduce(bf16[1536]{0:T(1024)(128)(2,1)S(1)} %get-tuple-element.47, bf16[1536]{0:T(1024)(128)(2,1)S(1)} %copy-done.24), channel_id=7, replica_groups=mesh['shard'=4,'ctx'=4,'tp'=2] {'shard'}, use_global_device_ids=true, to_apply=%region_13.14.clone | all-reduce | flops 3072 | bytes 12288
  814.9 10.1 all-reduce.2
  829.1 34.2 %all-reduce.13.cloned.1.call-done = (bf16[384,1,8,128]{3,0,2,1:T(8,128)(2,1)}, bf16[384,768]{1,0:T(8,128)(2,1)}) async-done(((bf16[384,1,8,128]{3,0,2,1:T(8,128)(2,1)}, bf16[384,768]{1,0:T(8,128)(2,1)}), (bf16[384,1,8,128]{3,0,2,1:T(8,128)(2,1)}, bf16[384,768]{1,0:T(8,128)(2,1)})) %all-reduce.13.cloned.1.call-update) | async-done | bytes 1376272 | tf_op jit(solution)/shard_map/psum | solution.py:219
  867.8 100.8 %all-gather.18.cloned.1.call-done = bf16[16,384,840]{1,2,0:T(8,128)(2,1)} async-done(((bf16[4,384,840]{1,2,0:T(8,128)(2,1)}), bf16[16,384,840]{1,2,0:T(8,128)(2,1)}) %all-gather.18.cloned.1.call-update) | async-done | bytes 10321936 | tf_op jit(solution)/shard_map/all_gather | solution.py:176
  968.6 12.6 %convert_multiply_fusion = f32[16,384,840]{1,2,0:T(8,128)} fusion(bf16[16,384,840]{1,2,0:T(8,128)(2,1)} %all-gather.18.cloned.1.call-done), kind=kLoop, calls=%fused_computation.1 | loop fusion | flops 10321920 | bytes 30965760 | tf_op jit(solution)/shard_map/mul | solution.py:179
  999.5 10.7 %slice.106 = f32[384,2,4480]{0,2,1:T(8,128)} slice(f32[384,3,4480]{0,2,1:T(8,128)} %bitcast.226), slice={[0:384], [0:2], [0:4480]} | slice | bytes 27525120 | tf_op jit(solution)/shard_map/slice | solution.py:229
  1010.2 21.5 %copy.86 = f32[384,2,4480]{2,1,0:T(2,128)} copy(f32[384,2,4480]{0,2,1:T(8,128)} %slice.106) | data formatting | bytes 27525120
  (209 shorter events, 145.7 us)
Async XLA Ops:
  7.2 69.9 %all-gather.10.cloned.1.call-start = ((), (), s32[]{:S(2)}) async-start(), calls=%async_computation.8 | async-start | bytes 3932160 | tf_op jit(solution)/shard_map/all_gather | solution.py:79
  9.8 117.6 %all-gather.12.cloned.1.call-start = ((), (), s32[]{:S(2)}) async-start(), calls=%async_computation.9 | async-start | bytes 2949120 | tf_op jit(solution)/shard_map/all_gather | solution.py:80
  10.5 138.2 %all-reduce.9.cloned.1.call-start = ((), (), s32[]{:S(2)}) async-start(), calls=%async_computation.10 | async-start | bytes 1572864 | tf_op jit(solution)/shard_map/psum | solution.py:46
  25.1 64.2 %copy-start.14 = (f32[128,128]{0,1:T(8,128)}, f32[128,128]{0,1:T(8,128)S(1)}, u32[]{:S(2)}) copy-start(f32[128,128]{0,1:T(8,128)S(1)} %get-tuple-element.85) | copy-start | bytes 196612
  25.1 64.2 %copy-start.17 = (f32[128,128]{0,1:T(8,128)}, f32[128,128]{0,1:T(8,128)S(1)}, u32[]{:S(2)}) copy-start(f32[128,128]{0,1:T(8,128)S(1)} %get-tuple-element.86) | copy-start | bytes 196612
  90.3 40.5 %copy-start.8 = (f32[6,128,512]{2,1,0:T(8,128)}, f32[6,128,512]{2,1,0:T(8,128)S(1)}, u32[]{:S(2)}) copy-start(f32[6,128,512]{2,1,0:T(8,128)S(1)} %get-tuple-element.84) | copy-start | bytes 4718596
  90.5 40.4 %copy-start.32 = (bf16[384]{0:T(512)(128)(2,1)S(1)}, bf16[384]{0:T(512)(128)(2,1)}, u32[]{:S(2)}) copy-start(bf16[384]{0:T(512)(128)(2,1)} %param.16) | copy-start | bytes 2308
  130.8 137.5 %all-gather.14.cloned.1.call-start = ((), (), s32[]{:S(2)}) async-start(), calls=%async_computation.11 | async-start | bytes 6488064 | tf_op jit(solution)/shard_map/all_gather | solution.py:153
  150.5 302.3 %copy-start.29 = (f32[128]{0:T(128)}, f32[128]{0:T(128)S(1)}, u32[]{:S(2)}) copy-start(f32[128]{0:T(128)S(1)} %get-tuple-element.82) | copy-start | bytes 1540
  151.4 168.9 %all-gather.16.cloned.1.call-start = ((), (), s32[]{:S(2)}) async-start(), calls=%async_computation.17 | async-start | bytes 6488064 | tf_op jit(solution)/shard_map/all_gather | solution.py:104
  152.2 298.3 %reduce-scatter.13.cloned.1.call-start = ((), (), s32[]{:S(2)}) async-start(), calls=%async_computation.13 | async-start | bytes 6488064 | tf_op jit(solution)/shard_map/reduce_scatter | solution.py:165
  336.8 233.9 %reduce-scatter.11.cloned.1.call-start = ((), (), s32[]{:S(2)}) async-start(), calls=%async_computation.12 | async-start | bytes 6488064 | tf_op jit(solution)/shard_map/reduce_scatter | solution.py:165
  344.6 259.3 %reduce-scatter.19.cloned.1.call-start = ((), (), s32[]{:S(2)}) async-start(), calls=%async_computation.19 | async-start | bytes 327680
  580.5 97.0 %reduce-scatter.17.cloned.1.call-start = ((), (), s32[]{:S(2)}) async-start(), calls=%async_computation.16 | async-start | bytes 2949120 | tf_op jit(solution)/shard_map/reduce_scatter | solution.py:216
  582.8 177.4 %reduce-scatter.15.cloned.1.call-start = ((), (), s32[]{:S(2)}) async-start(), calls=%async_computation.15 | async-start | bytes 3932160 | tf_op jit(solution)/shard_map/reduce_scatter | solution.py:216
  624.0 136.3 %all-to-all-start.1 = ((bf16[4,384,840]{1,2,0:T(8,128)(2,1)}), bf16[4,384,840]{1,2,0:T(8,128)(2,1)}, u32[]{:S(2)}, u32[]{:S(2)}) async-start(bf16[4,384,840]{1,2,0:T(8,128)(2,1)} %bitcast.230), calls=%async_computation.5 | async-start | bytes 5160960 | tf_op jit(solution)/shard_map/all_to_all | solution.py:175
  628.8 152.5 %reduce-scatter.21.cloned.1.call-start = ((), (), s32[]{:S(2)}) async-start(), calls=%async_computation.20 | async-start | bytes 40960
  631.6 169.6 %all-reduce.11.cloned.1.call-start = ((), (), s32[]{:S(2)}) async-start(), calls=%async_computation.14 | async-start | bytes 1572864 | tf_op jit(solution)/shard_map/psum | solution.py:46
  634.1 126.7 %copy-start.35 = (u32[32]{0:T(128)S(1)}, u32[32]{0:T(128)}, u32[]{:S(2)}) copy-start(u32[32]{0:T(128)} %constant.62) | copy-start | bytes 388
  634.2 229.1 %all-reduce.13.cloned.1.call-start = ((), (), s32[]{:S(2)}) async-start(), calls=%async_computation.21 | async-start | bytes 2752512 | tf_op jit(solution)/shard_map/psum | solution.py:219
  760.2 42.4 %copy-start.24 = (bf16[1536]{0:T(1024)(128)(2,1)S(1)}, bf16[1536]{0:T(1024)(128)(2,1)}, u32[]{:S(2)}) copy-start(bf16[1536]{0:T(1024)(128)(2,1)} %get-tuple-element.45) | copy-start | bytes 9220
  760.2 66.6 %copy-start.4 = (f32[128,1536]{1,0:T(8,128)S(1)}, f32[128,1536]{1,0:T(8,128)}, u32[]{:S(2)}) copy-start(f32[128,1536]{1,0:T(8,128)} %copy-done.3) | copy-start | bytes 2359300
  760.2 66.6 %copy-start.34 = (f32[128]{0:T(128)S(1)}, f32[128]{0:T(128)}, u32[]{:S(2)}) copy-start(f32[128]{0:T(128)} %get-tuple-element.79) | copy-start | bytes 1540
  760.2 208.4 %all-gather.18.cloned.1.call-start = ((), (), s32[]{:S(2)}) async-start(), calls=%async_computation.18 | async-start | bytes 12902400 | tf_op jit(solution)/shard_map/all_gather | solution.py:176
  (32 other events, 366.2 us)
Sparse Core Ops, SparseCore 0:
  10.2 66.9 all-gather.9
  78.7 48.5 all-gather.11
  130.9 17.7 all-reduce.8
  152.0 97.6 all-gather.13
  252.9 67.3 all-gather.15
  337.0 113.5 reduce-scatter.12
  456.7 113.9 reduce-scatter.10
  580.6 23.2 reduce-scatter.18
  606.2 71.1 reduce-scatter.16
  680.1 79.9 reduce-scatter.14
  763.0 18.2 reduce-scatter.20
  784.1 17.0 all-reduce.10
  804.3 58.8 all-reduce.12
  865.0 103.5 all-gather.17
